TPU v7x, 512 devices: a whole 4x8x8 slice. The times are simulated.
512 devices in a mesh: lat: 64 (over y_hi, x, z), ord: 8 (over y_lo, core).
Axes of the slice: x: 4, y: 8 (y_hi: 2, y_lo: 4; y = y_hi * 4 + y_lo), z: 8, core: 2. Of those that a mesh axis runs over, the one named last changes fastest.
Arguments:
- pressure: bfloat16 [2, 512, 5760], P(None, 'lat', 'ord'), may hold values from -6 to 6
- tables: bfloat16 [512, 512, 2048], P('ord', 'lat'), may hold values from -16 to 16
- quad_weight: float32 [512], replicated, may hold values from 0.5 to 2
- love_number: float32 [2048], replicated, may hold values from -0.5 to 0
- order_list: int32 [512], replicated, may hold values from 0 to 511, each once
- cycle_list: int32 [512], P('lat'), may hold values from 0 to 511, each once
Outputs:
- spectrum: float32 [2, 512, 2048], P(None, 'ord', 'lat')
- load_field: float32 [2, 512, 5760], P(None, 'lat', 'ord')
Inputs may be any that keep to these rules, and one draw needn't show every extreme that they name: `order_list`: every order from 0 to 511 stands in exactly one slot. `cycle_list`: every northern cycle from 0 to 511 stands in exactly one slot; the same slot of the southern half holds its mirror cycle.
All inputs are finite; a program needn't handle non-finite values.
Results may differ from a plain program's by a relative error of at most 0.0055.
Values may be sent and summed in bfloat16 or wider, within the bound.
A program may use at most 64 MiB of HBM per device.

v0:
```python
import functools
import math

import jax
import jax.numpy as jnp
from jax import lax
from jax.experimental import pallas as pl
from jax.experimental.pallas import tpu as pltpu
from jax.sharding import PartitionSpec as P

NLON = 5760
DENSITY_RATIO = 3.0 * 1025.0 / 5517.0
NY, NX, NZ = 2, 4, 8
LANES = 128
F32 = jnp.float32
BF16 = jnp.bfloat16


def dot(a, b, dims):
    return lax.dot_general(a, b, (dims, ((), ())), preferred_element_type=F32)


def turn(phase):
    quarter = NLON // 4
    q = jnp.floor(phase * (1.0 / quarter) + 0.5)
    x = (phase - q * quarter) * (2.0 * math.pi / NLON)
    q = q.astype(jnp.int32)
    z = x * x
    s = x + x * z * (-1.6666654611e-1 + z * (8.3321608736e-3 + z * -1.9515295891e-4))
    c = 1.0 - 0.5 * z + z * z * (4.166664568298827e-2 + z * (-1.388731625493765e-3 + z * 2.443315711809948e-5))
    odd = (q & 1) == 1
    cos = jnp.where(odd, s, c)
    sin = jnp.where(odd, c, s)
    cos = jnp.where(((q + 1) & 2) == 2, -cos, cos)
    return cos, jnp.where((q & 2) == 2, sin, -sin)


def kernel(
    sizes,
    p_ref,
    tab_hbm,
    qw_ref,
    love_ref,
    ord_ref,
    cyc_ref,
    spec_ref,
    field_ref,
    tab,
    trig,
    mcol,
    ptile,
    ssend,
    srecv,
    lhs,
    vbuf,
    xr,
    ubuf,
    zr,
    ysend,
    yr,
    coef,
    sgn,
    tab_sem,
    os_s,
    os_r,
    xs_s,
    xs_r,
    zs_s,
    zs_r,
    ys_s,
    ys_r,
    zg_s,
    zg_r,
    xg_s,
    xg_r,
    og_s,
    og_r,
):
    no, j, lon, ml, order_total, half_total, degrees = sizes
    rows = 2 * ml
    kk = ml * j
    run = degrees // (NY * NX)
    share = run // NZ
    blocks = -(-lon // LANES)
    lat = lax.axis_index("lat")
    me_o = lax.axis_index("ord")
    yh = lat // (NX * NZ)
    x = (lat // NZ) % NX
    z = lat % NZ

    def at(k_y, k_x, k_z):
        to = (((yh + k_y) % NY) * NX + (x + k_x) % NX) * NZ + (z + k_z) % NZ
        return {"lat": to}

    def send(src, dst, send_sem, recv_sem, device):
        copy = pltpu.make_async_remote_copy(
            src_ref=src,
            dst_ref=dst,
            send_sem=send_sem,
            recv_sem=recv_sem,
            device_id=device,
            device_id_type=pl.DeviceIdType.MESH,
        )
        copy.start()
        return copy

    peers = [{"ord": (me_o + k) % no} for k in range(1, no)]
    peers += [at(0, k, 0) for k in range(1, NX)]
    peers += [at(0, 0, k) for k in range(1, NZ)]
    peers += [at(1, 0, 0)]
    barrier = pltpu.get_barrier_semaphore()
    for peer in peers:
        pl.semaphore_signal(barrier, inc=1, device_id=peer, device_id_type=pl.DeviceIdType.MESH)

    tab_copy = pltpu.make_async_copy(tab_hbm, tab, tab_sem)
    tab_copy.start()

    width = ord_ref.shape[1]
    for g in range(ord_ref.shape[0]):
        line = ord_ref[g : g + 1, :].astype(F32)
        mcol[g * width : (g + 1) * width, :] = jnp.broadcast_to(line, (LANES, width)).T

    for h in range(2):
        ptile[h * j : (h + 1) * j, :] = jnp.zeros((j, blocks * LANES), F32)
        ptile[h * j : (h + 1) * j, :lon] = p_ref[h].astype(F32)
    grid_rows = ptile[...].astype(BF16)

    lane = lax.broadcasted_iota(jnp.int32, (8, LANES), 1).astype(F32)
    lon0 = (me_o * lon).astype(F32) + lane

    def make_group(g):
        m = mcol[pl.ds(pl.multiple_of(g * 8, 8), 8), :]
        c, s = turn(m * lon0)
        dc, ds = turn(m * float(LANES))
        at_row = pl.ds(pl.multiple_of(g * 16, 16), 16)
        for b in range(blocks):
            trig[at_row, b * LANES : (b + 1) * LANES] = jnp.concatenate([c, s], 0).astype(BF16)
            if b < blocks - 1:
                c, s = c * dc - s * ds, c * ds + s * dc

    ord_copies = []
    for k in [*range(1, no), 0]:
        to = (me_o + k) % no

        def two(i, carry, to=to):
            make_group(to * NZ + 2 * i)
            make_group(to * NZ + 2 * i + 1)
            return carry

        lax.fori_loop(0, NZ // 2, two, 0)
        part = dot(grid_rows, trig[pl.ds(pl.multiple_of(to * rows, rows), rows), :], ((1,), (1,)))
        if k == 0:
            own_part = part
            break
        ssend[k - 1] = part
        if k == 1:
            pl.semaphore_wait(barrier, len(peers))
        ord_copies.append(
            send(ssend.at[k - 1], srecv.at[k - 1], os_s.at[k - 1], os_r.at[k - 1], {"ord": to})
        )

    mloc = mcol[pl.ds(pl.multiple_of(me_o * ml, 8), ml), :]
    mrow = jnp.concatenate([mloc[8 * (i // 2) : 8 * (i // 2) + 8] for i in range(2 * NZ)], 0)
    mrow = jnp.concatenate([mrow] * (run // LANES), 1).astype(jnp.int32)
    run_lane = lax.broadcasted_iota(jnp.int32, (rows, run), 1)
    even = ((run_lane + mrow) & 1) == 0
    row_i = lax.broadcasted_iota(jnp.int32, (rows, kk), 0)
    col_i = lax.broadcasted_iota(jnp.int32, (rows, kk), 1)
    same_slot = (row_i // 16) * 8 + row_i % 8 == col_i // j
    pick_j = lax.broadcasted_iota(jnp.int32, (j, kk), 0)
    pick_c = lax.broadcasted_iota(jnp.int32, (j, kk), 1)
    pick = jnp.where(pick_j == pick_c % j, 1.0, 0.0).astype(BF16)

    row_j = lax.broadcasted_iota(jnp.int32, (j, rows), 0)
    weight = jnp.zeros((j, rows), F32)
    for i in range(j):
        weight = jnp.where(row_j == i, qw_ref[cyc_ref[i]], weight)
    weight = weight * (1.0 / math.sqrt(half_total))

    total = own_part
    for k in range(no - 1):
        ord_copies[k].wait_recv()
        total = total + srecv[k]
    total = total * (1.0 / math.sqrt(NLON))
    north, south = total[:j], total[j:]
    for i, folded in enumerate((weight * (north + south), weight * (north - south))):
        spread = dot(folded.T.astype(BF16), pick, ((1,), (0,)))
        lhs[i * rows : (i + 1) * rows, :] = jnp.where(same_slot, spread, 0.0).astype(BF16)

    tab_copy.wait()

    def degree_base(y, col):
        return pl.multiple_of(y * (NX * run) + col * run, run)

    def table_block(base):
        return tab[:, :, pl.ds(base, run)].reshape(kk, run)

    x_order = [2, 1, 3] if NX == 4 else [*range(1, NX)]
    z_order = sorted(range(1, NZ), key=lambda k: -min(k, NZ - k))
    x_copies = {}
    for kx in [*x_order, 0]:
        for y in range(NY):
            base = degree_base(y, (x + kx) % NX)
            prod = dot(lhs[...], table_block(base), ((1,), (0,)))
            value = jnp.where(even, prod[:rows], prod[rows:])
            value = jnp.where(run_lane + base >= mrow, value, 0.0)
            vbuf[kx, :, y * run : (y + 1) * run] = value.astype(BF16)
        if kx:
            for kz in [*z_order, 0]:
                piece = pl.ds(pl.multiple_of(((z + kz) % NZ) * 16, 16), 16)
                x_copies[kx, kz] = send(
                    vbuf.at[kx, piece],
                    xr.at[kx - 1, piece],
                    xs_s.at[kx - 1, kz],
                    xs_r.at[kx - 1, kz],
                    at(0, kx, 0),
                )

    z_copies = {}
    for kz in [*z_order, 0]:
        piece = pl.ds(pl.multiple_of(((z + kz) % NZ) * 16, 16), 16)
        summed = vbuf[0, piece, :].astype(F32)
        for kx in range(1, NX):
            x_copies[kx, kz].wait_recv()
            summed = summed + xr[kx - 1, piece, :].astype(F32)
        if kz:
            ubuf[kz - 1] = summed.astype(BF16)
            z_copies[kz] = send(
                ubuf.at[kz - 1], zr.at[kz - 1], zs_s.at[kz - 1], zs_r.at[kz - 1], at(0, 0, kz)
            )
    for kz in range(1, NZ):
        z_copies[kz].wait_recv()
        summed = summed + zr[kz - 1].astype(F32)
    ysend[...] = summed.astype(BF16)
    y_copy = send(ysend, yr, ys_s, ys_r, at(1, 0, 0))
    love = jnp.concatenate(
        [
            love_ref[pl.ds((y * NX * run + x * run) // LANES + i, 1), :]
            for y in range(NY)
            for i in range(run // LANES)
        ],
        1,
    )
    factor = DENSITY_RATIO * (1.0 + love)
    y_copy.wait_recv()
    summed = summed + yr[...].astype(F32)
    own_piece = pl.ds(pl.multiple_of(z * 16, 16), 16)
    coef[0, own_piece, :] = (factor * summed).astype(BF16)

    g_copies = []
    zg_copies = {}
    for kz in z_order:
        zg_copies[kz] = send(
            coef.at[0, own_piece], coef.at[0, own_piece], zg_s.at[kz - 1], zg_r.at[kz - 1], at(0, 0, kz)
        )
    for kz in [0, *reversed(z_order)]:
        piece = pl.ds(pl.multiple_of(((z + NZ - kz) % NZ) * 16, 16), 16)
        if kz:
            zg_copies[kz].wait_recv()
        for kx in x_order:
            g_copies.append(
                (
                    kx,
                    send(
                        coef.at[0, piece],
                        coef.at[kx, piece],
                        xg_s.at[kx - 1, kz],
                        xg_r.at[kx - 1, kz],
                        at(0, kx, 0),
                    ),
                )
            )

    synth = jnp.zeros((2 * rows, kk), F32)
    for kx in [0, *reversed(x_order)]:
        for k, copy in g_copies:
            if k == kx:
                copy.wait_recv()
        for y in range(NY):
            base = degree_base(y, (x + NX - kx) % NX)
            block = coef[kx, :, y * run : (y + 1) * run].astype(F32)
            both = jnp.concatenate([block, jnp.where(even, block, -block)], 0).astype(BF16)
            synth = synth + dot(both, table_block(base), ((1,), (1,)))

    halves = []
    for h in range(2):
        part = jnp.where(same_slot, synth[h * rows : (h + 1) * rows] * (1.0 / math.sqrt(degrees)), 0.0)
        halves.append(dot(pick, part.astype(BF16), ((1,), (1,))))
    sgn[0] = jnp.concatenate(halves, 0).astype(BF16)
    og_copies = [
        send(sgn.at[0], sgn.at[k], og_s.at[k - 1], og_r.at[k - 1], {"ord": (me_o + k) % no})
        for k in range(1, no)
    ]

    mine = coef[0, :, pl.ds(pl.multiple_of(yh * run, run), run)]
    sel_i = lax.broadcasted_iota(jnp.int32, (run, share), 0)
    sel_o = lax.broadcasted_iota(jnp.int32, (run, share), 1)
    sel = jnp.where(sel_i == sel_o + z * share, 1.0, 0.0)
    out = dot(mine, sel.astype(BF16), ((1,), (0,)))
    first = (yh * NX * run + x * run) // LANES
    love_run = jnp.concatenate([love_ref[pl.ds(first + i, 1), :] for i in range(run // LANES)], 1)
    own_factor = jnp.sum(jnp.where(sel > 0.5, (DENSITY_RATIO * (1.0 + love_run)).T, 0.0), 0, keepdims=True)
    out = out / own_factor
    for i in range(NZ):
        for c in range(2):
            spec_ref[c, i * 8 : (i + 1) * 8, :] = out[i * 16 + c * 8 : i * 16 + c * 8 + 8]

    field = jnp.zeros((2 * j, blocks * LANES), F32)
    for k in range(no):
        if k:
            og_copies[k - 1].wait_recv()
        source = (me_o + no - k) % no
        rows_of = pl.ds(pl.multiple_of(source * rows, rows), rows)
        field = field + dot(sgn[k], trig[rows_of, :], ((1,), (0,)))
    field = field * (1.0 / math.sqrt(order_total))
    for h in range(2):
        field_ref[h] = field[h * j : (h + 1) * j, :lon]

    for copy in [*ord_copies, *x_copies.values(), *z_copies.values(), y_copy, *zg_copies.values(), *og_copies]:
        copy.wait_send()
    for _, copy in g_copies:
        copy.wait_send()


def per_device(no, pressure, tables, quad_weight, love_number, order_list, cycle_list):
    j, lon = pressure.shape[1:]
    ml, _, degrees = tables.shape
    order_total = order_list.shape[0]
    rows = 2 * ml
    run = degrees // (NY * NX)
    lon_pad = -(-lon // LANES) * LANES
    width = min(LANES, order_total)
    sizes = (no, j, lon, ml, order_total, quad_weight.shape[0], degrees)
    vmem = pl.BlockSpec(memory_space=pltpu.VMEM)
    smem = pl.BlockSpec(memory_space=pltpu.SMEM)
    dma = pltpu.SemaphoreType.DMA
    spectrum, field = pl.pallas_call(
        functools.partial(kernel, sizes),
        out_shape=(
            jax.ShapeDtypeStruct((2, ml, run // NZ), F32),
            jax.ShapeDtypeStruct((2, j, lon), F32),
        ),
        in_specs=[vmem, pl.BlockSpec(memory_space=pl.ANY), smem, vmem, vmem, smem],
        out_specs=(vmem, vmem),
        scratch_shapes=[
            pltpu.VMEM((ml, j, degrees), BF16),
            pltpu.VMEM((no * rows, lon_pad), BF16),
            pltpu.VMEM((order_total, LANES), F32),
            pltpu.VMEM((2 * j, lon_pad), F32),
            pltpu.VMEM((no - 1, 2 * j, rows), F32),
            pltpu.VMEM((no - 1, 2 * j, rows), F32),
            pltpu.VMEM((2 * rows, ml * j), BF16),
            pltpu.VMEM((NX, rows, NY * run), BF16),
            pltpu.VMEM((NX - 1, rows, NY * run), BF16),
            pltpu.VMEM((NZ - 1, 16, NY * run), BF16),
            pltpu.VMEM((NZ - 1, 16, NY * run), BF16),
            pltpu.VMEM((16, NY * run), BF16),
            pltpu.VMEM((16, NY * run), BF16),
            pltpu.VMEM((NX, rows, NY * run), BF16),
            pltpu.VMEM((no, 2 * j, rows), BF16),
            dma,
            dma((no - 1,)),
            dma((no - 1,)),
            dma((NX - 1, NZ)),
            dma((NX - 1, NZ)),
            dma((NZ - 1,)),
            dma((NZ - 1,)),
            dma,
            dma,
            dma((NZ - 1,)),
            dma((NZ - 1,)),
            dma((NX - 1, NZ)),
            dma((NX - 1, NZ)),
            dma((no - 1,)),
            dma((no - 1,)),
        ],
        compiler_params=pltpu.CompilerParams(collective_id=0, has_side_effects=True),
        name="load_step",
    )(
        pressure,
        tables,
        quad_weight,
        love_number.reshape(-1, LANES),
        order_list.reshape(-1, width),
        cycle_list,
    )
    return spectrum, field


def solution(mesh):
    placed = (P(None, "lat", "ord"), P("ord", "lat", None), P(), P(), P(), P("lat"))
    return jax.shard_map(
        functools.partial(per_device, mesh.shape["ord"]),
        mesh=mesh,
        in_specs=placed,
        out_specs=(P(None, "ord", "lat"), P(None, "lat", "ord")),
        check_vma=False,
    )
```

profile of v0, /device:TPU:1, one launch (start us, length us, event | category | flops | bytes accessed | tf_op | source)
XLA Modules:
  0.0 58.7 jit_solution(12933732215348986999)
XLA Ops:
  0.6 55.1 %load_step.1 = (f32[2,64,32]{2,1,0:T(8,128)}, f32[2,8,720]{2,1,0:T(8,128)}) custom-call(bf16[2,8,720]{2,1,0:T(8,128)(2,1)} %p_ref.1, bf16[64,8,2048]{2,1,0:T(8,128)(2,1)} %tab_hbm.1, f32[512]{0:T(512)} %qw_ref.1, f32[16,128]{1,0:T(8,128)} %bitcast.2, s32[4,128]{1,0:T(4,128)} %bitcast.3, s32[8]{0:T(128)} %cyc_ref.1), custom_call_target="tpu_custom_call" | custom-call | tf_op jit(solution)/shard_map/load_step/pallas_call | solution.py:337
  55.7 1.5 %copy.8 = f32[2,64,32]{1,2,0:T(8,128)} copy(f32[2,64,32]{2,1,0:T(8,128)} %get-tuple-element.2) | data formatting | bytes 32768 | tf_op jit(solution)/shard_map/load_step/pallas_call | solution.py:337
  57.3 1.4 %copy.10 = f32[2,8,720]{2,1,0:T(8,128)} copy(f32[2,8,720]{2,1,0:T(8,128)} %get-tuple-element.7) | data formatting | bytes 92160
where the time goes:
time: 59 us; the launch traced here: 58.7 us
  Pallas kernels  55.1 us (93%)
  local copies, waits for them, and re-layouts  2.95 us (5%)
  between operations  0.64 us (1%)
    pallas_call x1, Pallas kernels, per_device(): pl.pallas_call(functools.partial(kernel, sizes), out_shape=(jax.ShapeDtyp...  55.1 us
    pallas_call x1, local copies, waits for them, and re-layouts, per_device(): pl.pallas_call(functools.partial(kernel, sizes), out_shape=(jax.ShapeDtyp...  1.53 us
    unnamed x1, local copies, waits for them, and re-layouts  1.42 us

commit v1 on v0

v1 whole, which is shorter than its diff:
```python
import functools
import math

import jax
import jax.numpy as jnp
from jax import lax
from jax.experimental import pallas as pl
from jax.experimental.pallas import tpu as pltpu
from jax.sharding import PartitionSpec as P

NLON = 5760
DENSITY_RATIO = 3.0 * 1025.0 / 5517.0
NY, NX, NZ = 2, 4, 8
LANES = 128
F32 = jnp.float32
BF16 = jnp.bfloat16


def dot(a, b, dims):
    return lax.dot_general(a, b, (dims, ((), ())), preferred_element_type=F32)


def turn(phase):
    quarter = NLON // 4
    q = jnp.floor(phase * (1.0 / quarter) + 0.5)
    x = (phase - q * quarter) * (2.0 * math.pi / NLON)
    q = q.astype(jnp.int32)
    z = x * x
    s = x + x * z * (-1.6666654611e-1 + z * (8.3321608736e-3 + z * -1.9515295891e-4))
    c = 1.0 - 0.5 * z + z * z * (4.166664568298827e-2 + z * (-1.388731625493765e-3 + z * 2.443315711809948e-5))
    odd = (q & 1) == 1
    cos = jnp.where(odd, s, c)
    sin = jnp.where(odd, c, s)
    cos = jnp.where(((q + 1) & 2) == 2, -cos, cos)
    return cos, jnp.where((q & 2) == 2, sin, -sin)


def kernel(
    sizes,
    p_hbm,
    tab_hbm,
    qw_hbm,
    love_hbm,
    ord_hbm,
    cyc_hbm,
    spec_ref,
    field_ref,
    p_ref,
    qw_ref,
    love_ref,
    ord_ref,
    cyc_ref,
    tab,
    trig,
    base,
    mcol,
    ptile,
    ssend,
    srecv,
    lhs,
    vbuf,
    xr,
    ubuf,
    zr,
    ysend,
    yr,
    coef,
    sgn,
    in_sem,
    os_s,
    os_r,
    xs_s,
    xs_r,
    zs_s,
    zs_r,
    ys_s,
    ys_r,
    zg_s,
    zg_r,
    xg_s,
    xg_r,
    og_s,
    og_r,
):
    no, j, lon, ml, order_total, half_total, degrees = sizes
    rows = 2 * ml
    kk = ml * j
    run = degrees // (NY * NX)
    share = run // NZ
    blocks = -(-lon // LANES)
    lat = lax.axis_index("lat")
    me_o = lax.axis_index("ord")
    yh = lat // (NX * NZ)
    x = (lat // NZ) % NX
    z = lat % NZ

    def at(k_y, k_x, k_z):
        to = (((yh + k_y) % NY) * NX + (x + k_x) % NX) * NZ + (z + k_z) % NZ
        return {"lat": to}

    def send(src, dst, send_sem, recv_sem, device):
        copy = pltpu.make_async_remote_copy(
            src_ref=src,
            dst_ref=dst,
            send_sem=send_sem,
            recv_sem=recv_sem,
            device_id=device,
            device_id_type=pl.DeviceIdType.MESH,
        )
        copy.start()
        return copy

    loads = {}
    for i, (name, src, dst) in enumerate(
        (
            ("ord", ord_hbm, ord_ref),
            ("p", p_hbm, p_ref),
            ("cyc", cyc_hbm, cyc_ref),
            ("qw", qw_hbm, qw_ref),
            ("love", love_hbm, love_ref),
            ("tab", tab_hbm, tab),
        )
    ):
        loads[name] = pltpu.make_async_copy(src, dst, in_sem.at[i])
        loads[name].start()

    peers = [{"ord": (me_o + k) % no} for k in range(1, no)]
    peers += [at(0, k, 0) for k in range(1, NX)]
    peers += [at(0, 0, k) for k in range(1, NZ)]
    peers += [at(1, 0, 0)]
    barrier = pltpu.get_barrier_semaphore()
    for peer in peers:
        pl.semaphore_signal(barrier, inc=1, device_id=peer, device_id_type=pl.DeviceIdType.MESH)

    loads["ord"].wait()
    order_f = ord_ref[...].astype(F32)
    width = order_f.shape[1]
    lines = [order_f[g : g + 1] for g in range(order_f.shape[0])]
    for g, line in enumerate(lines):
        mcol[g * width : (g + 1) * width, :] = jnp.broadcast_to(line, (LANES, width)).T
    m_lanes = jnp.concatenate(lines, 1)

    lane = lax.broadcasted_iota(jnp.int32, (16, LANES), 1).astype(F32)

    def make_base(g, carry):
        at_row = pl.multiple_of(g * 16, 16)
        for i, part in enumerate(turn(mcol[pl.ds(at_row, 16), :] * lane)):
            high = part.astype(BF16)
            base[pl.ds(i * order_total + at_row, 16), :LANES] = high
            base[pl.ds(i * order_total + at_row, 16), LANES:] = (part - high.astype(F32)).astype(BF16)
        return carry

    lax.fori_loop(0, order_total // 16, make_base, 0, unroll=4)

    loads["p"].wait()
    ptile[...] = jnp.zeros_like(ptile)
    for h in range(2):
        ptile[h * j : (h + 1) * j, :lon] = p_ref[h].astype(F32)
    split = jnp.concatenate([ptile[:, b * LANES : (b + 1) * LANES] for b in range(blocks)], 0)
    split = jnp.concatenate([split, split], 1).astype(BF16)
    first = dot(split, base[...], ((1,), (1,)))
    start = (lax.broadcasted_iota(jnp.int32, (blocks, order_total), 0) * LANES + me_o * lon).astype(F32)
    tc, ts = turn(m_lanes * start)
    re = im = 0.0
    for b in range(blocks):
        c = first[b * 2 * j : (b + 1) * 2 * j, :order_total]
        s = first[b * 2 * j : (b + 1) * 2 * j, order_total:]
        re = re + c * tc[b : b + 1] - s * ts[b : b + 1]
        im = im + c * ts[b : b + 1] + s * tc[b : b + 1]
    for d in range(no):
        cols = slice(d * ml, (d + 1) * ml)
        ssend[d] = jnp.concatenate([re[:, cols], im[:, cols]], 1)
    pl.semaphore_wait(barrier, len(peers))
    ord_copies = []
    for k in [*range(no // 2, no), *range(1, no // 2)]:
        to = (me_o + k) % no
        ord_copies.append(send(ssend.at[to], srecv.at[k - 1], os_s.at[k - 1], os_r.at[k - 1], {"ord": to}))

    lane8 = lax.broadcasted_iota(jnp.int32, (8, LANES), 1).astype(F32)
    lon0 = (me_o * lon).astype(F32) + lane8

    def make_group(g, carry):
        m = mcol[pl.ds(pl.multiple_of(g * 8, 8), 8), :]
        c, s = turn(m * lon0)
        dc, ds = turn(m * float(LANES))
        at_row = pl.ds(pl.multiple_of(g * 16, 16), 16)
        for b in range(blocks):
            trig[at_row, b * LANES : (b + 1) * LANES] = jnp.concatenate([c, s], 0).astype(BF16)
            if b < blocks - 1:
                c, s = c * dc - s * ds, c * ds + s * dc
        return carry

    lax.fori_loop(0, order_total // 8, make_group, 0, unroll=4)

    mloc = mcol[pl.ds(pl.multiple_of(me_o * ml, 8), ml), :]
    mrow = jnp.concatenate([mloc[8 * (i // 2) : 8 * (i // 2) + 8] for i in range(2 * NZ)], 0)
    mrow = jnp.concatenate([mrow] * (run // LANES), 1).astype(jnp.int32)
    run_lane = lax.broadcasted_iota(jnp.int32, (rows, run), 1)
    even = ((run_lane + mrow) & 1) == 0
    wide = NX * run
    wide_lane = lax.broadcasted_iota(jnp.int32, (8, wide), 1)
    row_i = lax.broadcasted_iota(jnp.int32, (rows, kk), 0)
    col_i = lax.broadcasted_iota(jnp.int32, (rows, kk), 1)
    same_slot = (row_i // 16) * 8 + row_i % 8 == col_i // j
    pick_j = lax.broadcasted_iota(jnp.int32, (j, kk), 0)
    pick_c = lax.broadcasted_iota(jnp.int32, (j, kk), 1)
    pick = jnp.where(pick_j == pick_c % j, 1.0, 0.0).astype(BF16)
    row_8 = lax.broadcasted_iota(jnp.int32, (rows, 8 * j), 0)
    col_8 = lax.broadcasted_iota(jnp.int32, (rows, 8 * j), 1)
    in_piece = row_8 % 8 == col_8 // j

    loads["cyc"].wait()
    loads["qw"].wait()
    row_j = lax.broadcasted_iota(jnp.int32, (j, rows), 0)
    weight = jnp.zeros((j, rows), F32)
    for i in range(j):
        weight = jnp.where(row_j == i, qw_ref[cyc_ref[i]], weight)
    weight = weight * (1.0 / math.sqrt(half_total))
    loads["love"].wait()
    loads["tab"].wait()

    total = ssend[me_o]
    for copy in ord_copies:
        copy.wait_recv()
    for k in range(no - 1):
        total = total + srecv[k]
    total = total * (1.0 / math.sqrt(NLON))
    north, south = total[:j], total[j:]
    for i, folded in enumerate((weight * (north + south), weight * (north - south))):
        spread = dot(folded.T.astype(BF16), pick[:, : 8 * j], ((1,), (0,)))
        spread = jnp.where(in_piece, spread, 0.0)
        for p in range(NZ):
            for c in range(2):
                lhs[p, (2 * i + c) * 8 : (2 * i + c) * 8 + 8, :] = spread[c * ml + p * 8 : c * ml + p * 8 + 8]

    x_order = [2, 1, 3] if NX == 4 else [*range(1, NX)]
    z_order = sorted(range(1, NZ), key=lambda k: -min(k, NZ - k))
    x_copies = {}
    for kz in [*z_order, 0]:
        zz = (z + kz) % NZ
        weights = lhs[zz].astype(BF16)
        m8 = mcol[pl.ds(pl.multiple_of(me_o * ml + zz * 8, 8), 8), :]
        m8 = jnp.concatenate([m8] * (wide // LANES), 1).astype(jnp.int32)
        even8 = ((wide_lane + m8) & 1) == 0
        for y in range(NY):
            block = tab[pl.ds(zz * 8, 8), :, y * wide : (y + 1) * wide].reshape(8 * j, wide)
            prod = dot(weights, block, ((1,), (0,)))
            present = wide_lane + y * wide >= m8
            value = [
                jnp.where(present, jnp.where(even8, prod[c * 8 : c * 8 + 8], prod[c * 8 + 16 : c * 8 + 24]), 0.0)
                for c in range(2)
            ]
            vbuf[kz, y] = jnp.concatenate(value, 0).astype(BF16)
        for kx in x_order:
            cols = pl.ds(pl.multiple_of(((x + kx) % NX) * run, run), run)
            x_copies[kx, kz] = send(
                vbuf.at[kz, :, :, cols],
                xr.at[kx - 1, kz],
                xs_s.at[kx - 1, kz],
                xs_r.at[kx - 1, kz],
                at(0, kx, 0),
            )

    own_cols = pl.ds(pl.multiple_of(x * run, run), run)
    z_copies = {}
    for kz in [*z_order, 0]:
        summed = vbuf[kz, :, :, own_cols].astype(F32)
        for kx in x_order:
            x_copies[kx, kz].wait_recv()
            summed = summed + xr[kx - 1, kz].astype(F32)
        if kz:
            ubuf[kz - 1] = summed.astype(BF16)
            z_copies[kz] = send(
                ubuf.at[kz - 1], zr.at[kz - 1], zs_s.at[kz - 1], zs_r.at[kz - 1], at(0, 0, kz)
            )
    for kz in z_order:
        z_copies[kz].wait_recv()
        summed = summed + zr[kz - 1].astype(F32)
    ysend[...] = summed.astype(BF16)
    y_copy = send(ysend, yr, ys_s, ys_r, at(1, 0, 0))
    def factor_of(y):
        at_love = (y * wide + x * run) // LANES
        return 1.0 + jnp.concatenate([love_ref[pl.ds(at_love + i, 1), :] for i in range(run // LANES)], 1)

    factors = [factor_of(y) for y in range(NY)]
    y_copy.wait_recv()
    summed = summed + yr[...].astype(F32)
    own_piece = pl.ds(pl.multiple_of(z * 16, 16), 16)
    for y in range(NY):
        coef[0, own_piece, y * run : (y + 1) * run] = (DENSITY_RATIO * factors[y] * summed[y]).astype(BF16)

    g_copies = []
    zg_copies = {}
    for kz in z_order:
        zg_copies[kz] = send(
            coef.at[0, own_piece], coef.at[0, own_piece], zg_s.at[kz - 1], zg_r.at[kz - 1], at(0, 0, kz)
        )
    for kz in [0, *reversed(z_order)]:
        piece = pl.ds(pl.multiple_of(((z + NZ - kz) % NZ) * 16, 16), 16)
        if kz:
            zg_copies[kz].wait_recv()
        for kx in x_order:
            g_copies.append(
                (
                    kx,
                    send(
                        coef.at[0, piece],
                        coef.at[kx, piece],
                        xg_s.at[kx - 1, kz],
                        xg_r.at[kx - 1, kz],
                        at(0, kx, 0),
                    ),
                )
            )

    synth = jnp.zeros((2 * rows, kk), F32)
    for kx in [0, *reversed(x_order)]:
        for k, copy in g_copies:
            if k == kx:
                copy.wait_recv()
        for y in range(NY):
            at_degree = pl.multiple_of(y * wide + ((x + NX - kx) % NX) * run, run)
            block = coef[kx, :, y * run : (y + 1) * run].astype(F32)
            both = jnp.concatenate([block, jnp.where(even, block, -block)], 0).astype(BF16)
            synth = synth + dot(both, tab[:, :, pl.ds(at_degree, run)].reshape(kk, run), ((1,), (1,)))

    halves = []
    for h in range(2):
        part = jnp.where(same_slot, synth[h * rows : (h + 1) * rows] * (1.0 / math.sqrt(degrees)), 0.0)
        halves.append(dot(pick, part.astype(BF16), ((1,), (1,))))
    sgn[0] = jnp.concatenate(halves, 0).astype(BF16)
    og_copies = [
        send(sgn.at[0], sgn.at[k], og_s.at[k - 1], og_r.at[k - 1], {"ord": (me_o + k) % no})
        for k in range(1, no)
    ]

    mine = coef[0, :, pl.ds(pl.multiple_of(yh * run, run), run)]
    sel_o = lax.broadcasted_iota(jnp.int32, (share, run), 0)
    sel_i = lax.broadcasted_iota(jnp.int32, (share, run), 1)
    sel = jnp.where(sel_i == sel_o + z * share, 1.0, 0.0)
    own_factor = jnp.sum(sel * factor_of(yh), 1, keepdims=True)
    out = dot(sel.astype(BF16), mine, ((1,), (1,))).astype(BF16)
    old = lax.broadcasted_iota(jnp.int32, (rows, rows), 0)
    new = lax.broadcasted_iota(jnp.int32, (rows, rows), 1)
    swap = old == ((new % ml) // 8) * 16 + (new // ml) * 8 + new % 8
    out = dot(out, jnp.where(swap, 1.0, 0.0).astype(BF16), ((1,), (0,)))
    out = out / own_factor
    for c in range(2):
        spec_ref[c] = out[:, c * ml : (c + 1) * ml]

    field = jnp.zeros((2 * j, blocks * LANES), F32)
    for k in range(no):
        if k:
            og_copies[k - 1].wait_recv()
        source = (me_o + no - k) % no
        rows_of = pl.ds(pl.multiple_of(source * rows, rows), rows)
        field = field + dot(sgn[k], trig[rows_of, :], ((1,), (0,)))
    for h in range(2):
        field_ref[h] = field[h * j : (h + 1) * j, :lon]

    for copy in [*ord_copies, *x_copies.values(), *z_copies.values(), y_copy, *zg_copies.values(), *og_copies]:
        copy.wait_send()
    for _, copy in g_copies:
        copy.wait_send()


def per_device(no, pressure, tables, quad_weight, love_number, order_list, cycle_list):
    j, lon = pressure.shape[1:]
    ml, _, degrees = tables.shape
    order_total = order_list.shape[0]
    rows = 2 * ml
    run = degrees // (NY * NX)
    share = run // NZ
    blocks = -(-lon // LANES)
    lon_pad = blocks * LANES
    width = min(LANES, order_total)
    sizes = (no, j, lon, ml, order_total, quad_weight.shape[0], degrees)
    vmem = pl.BlockSpec(memory_space=pltpu.VMEM)
    hbm = pl.BlockSpec(memory_space=pltpu.HBM)
    dma = pltpu.SemaphoreType.DMA
    spectrum, field = pl.pallas_call(
        functools.partial(kernel, sizes),
        out_shape=(
            jax.ShapeDtypeStruct((2, share, ml), F32),
            jax.ShapeDtypeStruct((2, j, lon), F32),
        ),
        in_specs=[hbm] * 6,
        out_specs=(vmem, vmem),
        scratch_shapes=[
            pltpu.VMEM((2, j, lon), BF16),
            pltpu.SMEM(quad_weight.shape, F32),
            pltpu.VMEM((degrees // LANES, LANES), F32),
            pltpu.VMEM((order_total // width, width), jnp.int32),
            pltpu.SMEM(cycle_list.shape, jnp.int32),
            pltpu.VMEM((ml, j, degrees), BF16),
            pltpu.VMEM((no * rows, lon_pad), BF16),
            pltpu.VMEM((2 * order_total, 2 * LANES), BF16),
            pltpu.VMEM((order_total, LANES), F32),
            pltpu.VMEM((2 * j, lon_pad), F32),
            pltpu.VMEM((no, 2 * j, rows), F32),
            pltpu.VMEM((no - 1, 2 * j, rows), F32),
            pltpu.VMEM((NZ, 32, 8 * j), F32),
            pltpu.VMEM((NZ, NY, 16, NX * run), BF16),
            pltpu.VMEM((NX - 1, NZ, NY, 16, run), BF16),
            pltpu.VMEM((NZ - 1, NY, 16, run), BF16),
            pltpu.VMEM((NZ - 1, NY, 16, run), BF16),
            pltpu.VMEM((NY, 16, run), BF16),
            pltpu.VMEM((NY, 16, run), BF16),
            pltpu.VMEM((NX, rows, NY * run), BF16),
            pltpu.VMEM((no, 2 * j, rows), BF16),
            dma((6,)),
            dma((no - 1,)),
            dma((no - 1,)),
            dma((NX - 1, NZ)),
            dma((NX - 1, NZ)),
            dma((NZ - 1,)),
            dma((NZ - 1,)),
            dma,
            dma,
            dma((NZ - 1,)),
            dma((NZ - 1,)),
            dma((NX - 1, NZ)),
            dma((NX - 1, NZ)),
            dma((no - 1,)),
            dma((no - 1,)),
        ],
        compiler_params=pltpu.CompilerParams(
            collective_id=0, has_side_effects=True, vmem_limit_bytes=24 * 1024 * 1024
        ),
        name="load_step",
    )(
        *(
            pltpu.with_memory_space_constraint(v, pltpu.HBM)
            for v in (
                pressure,
                tables,
                quad_weight,
                love_number.reshape(-1, LANES),
                order_list.reshape(-1, width),
                cycle_list,
            )
        )
    )
    return (jnp.swapaxes((1.0 / DENSITY_RATIO) * spectrum, 1, 2), (1.0 / math.sqrt(order_total)) * field)


def solution(mesh):
    placed = (P(None, "lat", "ord"), P("ord", "lat", None), P(), P(), P(), P("lat"))
    return jax.shard_map(
        functools.partial(per_device, mesh.shape["ord"]),
        mesh=mesh,
        in_specs=placed,
        out_specs=(P(None, "ord", "lat"), P(None, "lat", "ord")),
        check_vma=False,
    )
```

time: 59 us -> 52.1 us (0.88)
  Pallas kernels: 55.1 us -> 50.1 us
  local copies, waits for them, and re-layouts: 2.95 us -> 0 us
  other arithmetic: 0 us -> 1.24 us
    pallas_call x1, Pallas kernels: 55.1 us -> 50.1 us  [per_device(): pl.pallas_call(functools.partial(kernel, sizes), out_shape=(jax.ShapeDtyp...]
    pallas_call x1 -> x0, local copies, waits for them, and re-layouts: 1.53 us -> none  [per_device(): pl.pallas_call(functools.partial(kernel, sizes), out_shape=(jax.ShapeDtyp...]
    unnamed x1 -> x0, local copies, waits for them, and re-layouts: 1.42 us -> none
    mul x0 -> x1, other arithmetic: none -> 0.62 us  [per_device(): 1.0 / math.sqrt(order_total) * field]
    transpose x0 -> x1, other arithmetic: none -> 0.62 us  [per_device(): jnp.swapaxes(1.0 / DENSITY_RATIO * spectrum, 1, 2)]
where the time goes in v1:
time: 52.1 us; the launch traced here: 52 us
  Pallas kernels  50.1 us (96%)
  other arithmetic  1.24 us (2%)
  between operations  0.64 us (1%)
    pallas_call x1, Pallas kernels, per_device(): pl.pallas_call(functools.partial(kernel, sizes), out_shape=(jax.ShapeDtyp...  50.1 us

profile of v1, /device:TPU:1, one launch (start us, length us, event | category | flops | bytes accessed | tf_op | source)
XLA Modules:
  0.0 52.0 jit_solution(2919267152172726211)
XLA Ops:
  0.6 50.1 %load_step.1 = (f32[2,32,64]{2,1,0:T(8,128)S(1)}, f32[2,8,720]{2,1,0:T(8,128)S(1)}) custom-call(bf16[2,8,720]{2,1,0:T(8,128)(2,1)} %p_hbm.1, bf16[64,8,2048]{2,1,0:T(8,128)(2,1)} %tab_hbm.1, f32[512]{0:T(512)} %qw_hbm.1, f32[16,128]{1,0:T(8,128)} %bitcast.4, s32[4,128]{1,0:T(4,128)} %bitcast.5, s32[8]{0:T(128)} %cyc_hbm.1), custom_call_target="tpu_custom_call" | custom-call | tf_op jit(solution)/shard_map/load_step/pallas_call | solution.py:381
  50.7 0.6 %multiply_bitcast_fusion = f32[2,64,32]{1,2,0:T(8,128)} fusion(f32[2,32,64]{2,1,0:T(8,128)S(1)} %get-tuple-element.4), kind=kLoop, calls=%fused_computation | loop fusion | flops 4096 | bytes 32768 | tf_op jit(solution)/shard_map/transpose | solution.py:444
  51.4 0.6 %broadcast_multiply_fusion = f32[2,8,720]{2,1,0:T(8,128)} fusion(f32[2,8,720]{2,1,0:T(8,128)S(1)} %get-tuple-element.5), kind=kLoop, calls=%fused_computation.1 | loop fusion | flops 11520 | bytes 92160 | tf_op jit(solution)/shard_map/mul | solution.py:444
